TPU v7x, 32 devices: a whole 2x2x4 slice. The times are simulated.
32 devices in a mesh: ctx: 4 (over y, x), head: 8 (over z, core).
Axes of the slice: x: 2, y: 2, z: 4, core: 2. Of those that a mesh axis runs over, the one named last changes fastest.
Arguments:
- state: bfloat16 [4096, 2048], P('ctx'), may hold values from -6 to 6
- norm_gain: bfloat16 [2048], replicated, may hold values from 0.5 to 1.5
- w_qkv: bfloat16 [3, 2048, 2048], P(None, None, 'head'), may hold values from -2 to 2
- w_out: bfloat16 [2048, 2048], P('head'), may hold values from -0.125 to 0.125
- probe: bfloat16 [4096, 2048], P('ctx'), may hold values from -6 to 6
- noise: bfloat16 [4096, 2048], P(('ctx', 'head')), may hold values from -6 to 6
- segment_ids: int32 [4096], P('ctx'), may hold values from 0 to 2, never falling along the last dimension, each value on 1 to 3072 neighbouring positions
Outputs:
- new_state: float32 [4096, 2048], P(('ctx', 'head'))
Inputs may be any that keep to these rules, and one draw needn't show every extreme that they name: `segment_ids`: segment numbers never fall along the sequence; a segment holds at most 3072 positions.
All inputs are finite; a program needn't handle non-finite values.
Results may differ from a plain program's by a relative error of at most 0.011.
Values may be sent and summed in bfloat16 or wider, within the bound.
A program may use at most 128 MiB of HBM per device.

v0:
```python
import jax
import jax.numpy as jnp
from jax import lax
from jax.sharding import PartitionSpec as P

HEAD_DIM = 128
EPSILON = 1e-05
STEP_SIZE = 0.25
NEGATIVE = -1e30


def row_scale(matrix):
    return lax.rsqrt(jnp.mean(matrix * matrix, axis=-1, keepdims=True) + EPSILON)


def readout_grad(layer_out, probe_full):
    scale_y = row_scale(layer_out)
    return scale_y * probe_full - layer_out * scale_y**3 * jnp.mean(
        probe_full * layer_out, axis=-1, keepdims=True
    )


def over_blocks(block_fn, state_carry, arrays, begin_row, block_limit):
    row_count = arrays[0].shape[0]
    block_size = min(row_count, block_limit)
    number = row_count // block_size
    stacked = tuple((member.reshape((number, block_size) + member.shape[1:]) for member in arrays))
    offsets = begin_row + block_size * jnp.arange(number, dtype=jnp.int32)

    def advance(running, scan_item):
        return (block_fn(running, scan_item[0], scan_item[1]), None)

    state_carry, _ = lax.scan(advance, state_carry, (stacked, offsets))
    return state_carry


def body(state, norm_gain, w_qkv, w_out, probe, noise, segment_ids):
    local_rows, model_width = state.shape
    local_heads = w_qkv.shape[2] // HEAD_DIM
    score_scale = HEAD_DIM ** (-0.5)
    head_count = lax.axis_size("head")
    ctx_index = lax.axis_index("ctx")
    own_rows = local_rows // head_count
    row_start = lax.axis_index("head") * own_rows
    state_f = state.astype(jnp.float32)
    gain_full = norm_gain.astype(jnp.float32)
    inverse = row_scale(state_f)
    normed = (state_f * inverse * gain_full).astype(jnp.bfloat16)
    projected = jnp.einsum("sd,cdn->csn", normed, w_qkv, preferred_element_type=jnp.float32).astype(
        jnp.bfloat16
    )
    query_rows, key_rows, value_rows = (projected[0], projected[1], projected[2])
    queries = query_rows.reshape(local_rows, local_heads, HEAD_DIM).transpose(1, 0, 2)
    query_pos = ctx_index * local_rows + jnp.arange(local_rows, dtype=jnp.int32)

    def visible(key_seg, key_start):
        key_pos = key_start + jnp.arange(key_seg.shape[0], dtype=jnp.int32)
        return (
            (key_pos[None, :] <= query_pos[:, None]) & (key_seg[None, :] == segment_ids[:, None])
        )[None]

    def forward_block(state_carry, key_piece, key_start):
        run_max, run_sum, run_acc = state_carry
        block_rows = key_piece[0].shape[0]
        key_heads = key_piece[0].reshape(block_rows, local_heads, HEAD_DIM)
        value_heads = key_piece[1].reshape(block_rows, local_heads, HEAD_DIM)
        allowed = visible(key_piece[2], key_start)
        scores = (
            jnp.einsum("hqe,khe->hqk", queries, key_heads, preferred_element_type=jnp.float32)
            * score_scale
        )
        scores = jnp.where(allowed, scores, NEGATIVE)
        new_max = jnp.maximum(run_max, jnp.max(scores, axis=-1))
        weights = jnp.where(allowed, jnp.exp(scores - new_max[..., None]), 0.0)
        factor = jnp.exp(run_max - new_max)
        run_sum = run_sum * factor + jnp.sum(weights, axis=-1)
        run_acc = run_acc * factor[..., None] + jnp.einsum(
            "hqk,khe->hqe",
            weights.astype(jnp.bfloat16),
            value_heads,
            preferred_element_type=jnp.float32,
        )
        return (new_max, run_sum, run_acc)

    initial = (
        jnp.full((local_heads, local_rows), NEGATIVE, jnp.float32),
        jnp.zeros((local_heads, local_rows), jnp.float32),
        jnp.zeros((local_heads, local_rows, HEAD_DIM), jnp.float32),
    )
    all_keys, all_values, all_segs = (
        lax.all_gather(key_rows, "ctx", axis=0, tiled=True),
        lax.all_gather(value_rows, "ctx", axis=0, tiled=True),
        lax.all_gather(segment_ids, "ctx", axis=0, tiled=True),
    )
    run_max, run_sum, run_acc = over_blocks(
        forward_block, initial, (all_keys, all_values, all_segs), 0, local_rows
    )
    outputs = (run_acc / run_sum[..., None]).astype(jnp.bfloat16)
    log_totals = run_max + jnp.log(run_sum)
    out_rows = outputs.transpose(1, 0, 2).reshape(local_rows, local_heads * HEAD_DIM)
    state_own = lax.dynamic_slice_in_dim(state_f, row_start, own_rows, 0)
    inverse_own = lax.dynamic_slice_in_dim(inverse, row_start, own_rows, 0)
    term = jnp.dot(out_rows, w_out, preferred_element_type=jnp.float32)
    layer_out = state_f + lax.psum(term.astype(jnp.bfloat16), "head").astype(jnp.float32)
    readout_full = readout_grad(layer_out, probe.astype(jnp.float32))
    readout_half = readout_full.astype(jnp.bfloat16)
    readout_own = lax.dynamic_slice_in_dim(readout_full, row_start, own_rows, 0)
    grads_out = jnp.einsum(
        "sd,hed->hse",
        readout_half,
        w_out.reshape(local_heads, HEAD_DIM, model_width),
        preferred_element_type=jnp.float32,
    ).astype(jnp.bfloat16)
    deltas = jnp.sum(grads_out.astype(jnp.float32) * outputs.astype(jnp.float32), axis=-1)

    def back_block(key_block, value_block, seg_block, key_start):
        block_rows = key_block.shape[0]
        key_heads = key_block.reshape(block_rows, local_heads, HEAD_DIM)
        value_heads = value_block.reshape(block_rows, local_heads, HEAD_DIM)
        allowed = visible(seg_block, key_start)
        scores = (
            jnp.einsum("hqe,khe->hqk", queries, key_heads, preferred_element_type=jnp.float32)
            * score_scale
        )
        probabilities = jnp.where(
            allowed, jnp.exp(jnp.where(allowed, scores, NEGATIVE) - log_totals[..., None]), 0.0
        )
        dprobs = jnp.einsum(
            "hqe,khe->hqk", grads_out, value_heads, preferred_element_type=jnp.float32
        )
        dscores = probabilities * (dprobs - deltas[..., None])
        prob_half = probabilities.astype(jnp.bfloat16)
        dscore_half = dscores.astype(jnp.bfloat16)
        value_part = jnp.einsum(
            "hqk,hqe->khe", prob_half, grads_out, preferred_element_type=jnp.float32
        )
        key_part = (
            jnp.einsum("hqk,hqe->khe", dscore_half, queries, preferred_element_type=jnp.float32)
            * score_scale
        )
        query_part = (
            jnp.einsum("hqk,khe->hqe", dscore_half, key_heads, preferred_element_type=jnp.float32)
            * score_scale
        )
        return (query_part, key_part.reshape(block_rows, -1), value_part.reshape(block_rows, -1))

    query_zero = jnp.zeros((local_heads, local_rows, HEAD_DIM), jnp.float32)

    def add_query(running, key_piece, key_start):
        query_part, _, _ = back_block(key_piece[0], key_piece[1], key_piece[2], key_start)
        return running + query_part

    query_acc = over_blocks(add_query, query_zero, (all_keys, all_values, all_segs), 0, local_rows)
    row_count = local_rows * lax.axis_size("ctx")
    block_size = min(row_count, local_rows)
    number = row_count // block_size

    def one_block(block_index):
        offset = block_index * block_size
        key_block = lax.dynamic_slice_in_dim(all_keys, offset, block_size, 0)
        value_block = lax.dynamic_slice_in_dim(all_values, offset, block_size, 0)
        seg_block = lax.dynamic_slice_in_dim(all_segs, offset, block_size, 0)
        _, key_part, value_part = back_block(key_block, value_block, seg_block, offset)
        return jnp.concatenate([key_part, value_part], axis=1)

    part_rows = lax.map(one_block, jnp.arange(number, dtype=jnp.int32))
    summed = lax.psum_scatter(
        part_rows.reshape(row_count, -1).astype(jnp.bfloat16),
        "ctx",
        scatter_dimension=0,
        tiled=True,
    ).astype(jnp.float32)
    key_sum = summed[:, : local_heads * HEAD_DIM]
    value_sum = summed[:, local_heads * HEAD_DIM :]
    query_grad = (
        query_acc.astype(jnp.bfloat16)
        .transpose(1, 0, 2)
        .reshape(local_rows, local_heads * HEAD_DIM)
    )
    key_grad = key_sum.astype(jnp.bfloat16)
    value_grad = value_sum.astype(jnp.bfloat16)
    running = jnp.einsum("sn,dn->sd", query_grad, w_qkv[0], preferred_element_type=jnp.float32)
    running = running + jnp.einsum(
        "sn,dn->sd", key_grad, w_qkv[1], preferred_element_type=jnp.float32
    )
    normed_grad = lax.psum_scatter(
        (
            running
            + jnp.einsum("sn,dn->sd", value_grad, w_qkv[2], preferred_element_type=jnp.float32)
        ).astype(jnp.bfloat16),
        "head",
        scatter_dimension=0,
        tiled=True,
    ).astype(jnp.float32)
    gain_grad = normed_grad * gain_full
    gradient = (
        readout_own
        + inverse_own * gain_grad
        - state_own * inverse_own**3 * jnp.mean(gain_grad * state_own, axis=-1, keepdims=True)
    )
    return state_own - STEP_SIZE * gradient + jnp.sqrt(2.0 * STEP_SIZE) * noise.astype(jnp.float32)


def solution(mesh):
    placed = (
        P("ctx", None),
        P(),
        P(None, None, "head"),
        P("head", None),
        P("ctx", None),
        P(("ctx", "head"), None),
        P("ctx"),
    )
    return jax.shard_map(
        body, mesh=mesh, in_specs=placed, out_specs=P(("ctx", "head"), None), check_vma=False
    )
```

profile of v0, /device:TPU:0, one launch (start us, length us, event | category | flops | bytes accessed | tf_op | source)
XLA Modules:
  0.0 553.4 jit_solution(13009157587223237203)
XLA Ops:
  10.4 6.9 %fusion.73 = bf16[3,1024,256]{1,2,0:T(8,128)(2,1)S(1)} fusion(bf16[3,2048,256]{2,1,0:T(8,128)(2,1)} %param.15, bf16[1024,2048]{1,0:T(8,128)(2,1)} %param.13, f32[2048]{0:T(1024)S(1)} %convert_element_type.76, f32[1024]{0:T(1024)S(1)} %add_rsqrt_fusion.1), kind=kOutput, calls=%fused_computation.90 | convolution fusion | flops 3230400512 | bytes 8925184 | tf_op jit(solution)/shard_map/sd,cdn->csn/dot_general | solution.py:49
  19.6 10.0 %all_gather.9 = s32[4096]{0:T(1024)S(1)} all-gather(s32[1024]{0:T(1024)S(1)} %copy-done.10), channel_id=1, replica_groups=mesh['ctx'=4,'head'=8] {'ctx'}, dimensions={0}, use_global_device_ids=true | all-gather | bytes 20480 | tf_op jit(solution)/shard_map/all_gather | solution.py:93
  29.6 26.9 %all-gather.5.cloned.1.call-done = bf16[1,4096,256]{1,2,0:T(8,128)(2,1)} async-done(((bf16[1,1024,256]{1,2,0:T(8,128)(2,1)}), bf16[1,4096,256]{1,2,0:T(8,128)(2,1)}) %all-gather.5.cloned.1.call-update) | async-done | bytes 2097168 | tf_op jit(solution)/shard_map/all_gather | solution.py:91
  56.6 4.5 reshape.283
  64.7 28.9 %all-gather.7.cloned.1.call-done = bf16[1,4096,256]{1,2,0:T(8,128)(2,1)} async-done(((bf16[1,1024,256]{1,2,0:T(8,128)(2,1)}), bf16[1,4096,256]{1,2,0:T(8,128)(2,1)}) %all-gather.7.cloned.1.call-update) | async-done | bytes 2097168 | tf_op jit(solution)/shard_map/all_gather | solution.py:92
  93.6 4.5 reshape.284
  98.2 3.6 copy.82
  101.7 83.2 %while.38 = (s32[]{:T(128)}, f32[2,1024]{1,0:T(2,128)S(1)}, f32[2,1024]{1,0:T(2,128)S(1)}, f32[2,1024,128]{2,1,0:T(8,128)}, s32[4]{0:T(128)S(1)}, /*index=5*/s32...) while((s32[]{:T(128)}, f32[2,1024]{1,0:T(2,128)S(1)}, ...), condition=%wide.region_4.5_spmd.clone, body=%wide.region_1.4_spmd.clone.sunk | while | flops 1104949248 | bytes 70942944 | solution.py:33
  106.4 5.1 fusion.158
  111.5 4.7 fusion.160
  117.4 4.4 fusion.162
  126.4 5.1 fusion.158
  131.5 4.7 fusion.160
  137.4 5.4 fusion.162
  147.5 5.1 fusion.158
  152.6 4.7 fusion.160
  158.5 5.4 fusion.162
  168.6 5.1 fusion.158
  173.6 4.7 fusion.160
  179.5 5.4 fusion.162
  192.7 96.0 %all-reduce.2.cloned.1.call-done = bf16[1024,2048]{1,0:T(8,128)(2,1)} async-done(((bf16[1024,2048]{1,0:T(8,128)(2,1)}), bf16[1024,2048]{1,0:T(8,128)(2,1)}) %all-reduce.2.cloned.1.call-update) | async-done | bytes 4194320 | tf_op jit(solution)/shard_map/psum | solution.py:104
  288.7 6.0 %multiply_reduce_fusion = (f32[1024]{0:T(1024)S(1)}, f32[1024]{0:T(1024)S(1)}) fusion(bf16[1024,2048]{1,0:T(8,128)(2,1)} %all-reduce.2.cloned.1.call-done, bf16[1024,2048]{1,0:T(8,128)(2,1)} %param.13, bf16[1024,2048]{1,0:T(8,128)(2,1)} %param.17), kind=kLoop, calls=%fused_computation.77 | loop fusion | flops 16775168 | bytes 12591104 | tf_op jit(solution)/shard_map/reduce_sum | solution.py:13
  307.1 97.3 %while.37 = (s32[]{:T(128)}, bf16[4,1024,512]{2,1,0:T(8,128)(2,1)}, s32[4]{0:T(128)S(1)}, s32[4096]{0:T(1024)S(1)}, s32[1024]{0:T(1024)S(1)}, /*index=5*/bf16[40...) while((s32[]{:T(128)}, bf16[4,1024,512]{2,1,0:T(8,128)(2,1)}, ...), condition=%wide.region_12.13_spmd.clone, body=%wide.region_11.12_spmd.clone.sunk | while | flops 2178418688 | bytes 40952544 | solution.py:166
  310.9 4.5 fusion.151
  315.4 8.0 %fusion.153 = bf16[2,1024,128]{1,2,0:T(8,128)(2,1)S(1)} fusion(bf16[2,1024,128]{1,2,0:T(8,128)(2,1)S(1)} %get-tuple-element.903, f32[2,1024,1024]{2,1,0:T(8,128)} %fusion.151, f32[2,1024]{1,0:T(2,128)S(1)} %get-tuple-element.907, f32[2,1024]{1,0:T(2,128)S(1)} %get-tuple-element.904, pred[1024,1024]{0,1:T(8,128)(4,1)S(1)} %compare_and_fusion.6, ...), kind=kOutput, calls=%fused_computation.17.clone.1 | convolution fusion | flops 1088946176 | bytes 11550720 | tf_op jit(solution)/shard_map/while/body/eval_jaxpr/hqk,hqe->khe/dot_general | solution.py:138
  323.4 6.3 %fusion.152 = bf16[2,1024,128]{1,2,0:T(8,128)(2,1)S(1)} fusion(bf16[2,1024,128]{1,2,0:T(8,128)(2,1)} %get-tuple-element.906, f32[2,1024,1024]{2,1,0:T(8,128)} %fusion.151, f32[2,1024]{1,0:T(2,128)S(1)} %get-tuple-element.904, pred[1024,1024]{0,1:T(8,128)(4,1)S(1)} %compare_and_fusion.6), kind=kOutput, calls=%fused_computation.10.clone.1 | convolution fusion | flops 547356672 | bytes 10493952 | tf_op jit(solution)/shard_map/while/body/eval_jaxpr/hqk,hqe->khe/dot_general | solution.py:134
  335.2 4.5 fusion.151
  339.7 8.0 %fusion.153 = bf16[2,1024,128]{1,2,0:T(8,128)(2,1)S(1)} fusion(bf16[2,1024,128]{1,2,0:T(8,128)(2,1)S(1)} %get-tuple-element.903, f32[2,1024,1024]{2,1,0:T(8,128)} %fusion.151, f32[2,1024]{1,0:T(2,128)S(1)} %get-tuple-element.907, f32[2,1024]{1,0:T(2,128)S(1)} %get-tuple-element.904, pred[1024,1024]{0,1:T(8,128)(4,1)S(1)} %compare_and_fusion.6, ...), kind=kOutput, calls=%fused_computation.17.clone.1 | convolution fusion | flops 1088946176 | bytes 11550720 | tf_op jit(solution)/shard_map/while/body/eval_jaxpr/hqk,hqe->khe/dot_general | solution.py:138
  347.7 6.3 %fusion.152 = bf16[2,1024,128]{1,2,0:T(8,128)(2,1)S(1)} fusion(bf16[2,1024,128]{1,2,0:T(8,128)(2,1)} %get-tuple-element.906, f32[2,1024,1024]{2,1,0:T(8,128)} %fusion.151, f32[2,1024]{1,0:T(2,128)S(1)} %get-tuple-element.904, pred[1024,1024]{0,1:T(8,128)(4,1)S(1)} %compare_and_fusion.6), kind=kOutput, calls=%fused_computation.10.clone.1 | convolution fusion | flops 547356672 | bytes 10493952 | tf_op jit(solution)/shard_map/while/body/eval_jaxpr/hqk,hqe->khe/dot_general | solution.py:134
  359.5 4.5 fusion.151
  364.1 8.0 %fusion.153 = bf16[2,1024,128]{1,2,0:T(8,128)(2,1)S(1)} fusion(bf16[2,1024,128]{1,2,0:T(8,128)(2,1)S(1)} %get-tuple-element.903, f32[2,1024,1024]{2,1,0:T(8,128)} %fusion.151, f32[2,1024]{1,0:T(2,128)S(1)} %get-tuple-element.907, f32[2,1024]{1,0:T(2,128)S(1)} %get-tuple-element.904, pred[1024,1024]{0,1:T(8,128)(4,1)S(1)} %compare_and_fusion.6, ...), kind=kOutput, calls=%fused_computation.17.clone.1 | convolution fusion | flops 1088946176 | bytes 11550720 | tf_op jit(solution)/shard_map/while/body/eval_jaxpr/hqk,hqe->khe/dot_general | solution.py:138
  372.1 6.3 %fusion.152 = bf16[2,1024,128]{1,2,0:T(8,128)(2,1)S(1)} fusion(bf16[2,1024,128]{1,2,0:T(8,128)(2,1)} %get-tuple-element.906, f32[2,1024,1024]{2,1,0:T(8,128)} %fusion.151, f32[2,1024]{1,0:T(2,128)S(1)} %get-tuple-element.904, pred[1024,1024]{0,1:T(8,128)(4,1)S(1)} %compare_and_fusion.6), kind=kOutput, calls=%fused_computation.10.clone.1 | convolution fusion | flops 547356672 | bytes 10493952 | tf_op jit(solution)/shard_map/while/body/eval_jaxpr/hqk,hqe->khe/dot_general | solution.py:134
  383.8 4.5 fusion.151
  388.3 8.0 %fusion.153 = bf16[2,1024,128]{1,2,0:T(8,128)(2,1)S(1)} fusion(bf16[2,1024,128]{1,2,0:T(8,128)(2,1)S(1)} %get-tuple-element.903, f32[2,1024,1024]{2,1,0:T(8,128)} %fusion.151, f32[2,1024]{1,0:T(2,128)S(1)} %get-tuple-element.907, f32[2,1024]{1,0:T(2,128)S(1)} %get-tuple-element.904, pred[1024,1024]{0,1:T(8,128)(4,1)S(1)} %compare_and_fusion.6, ...), kind=kOutput, calls=%fused_computation.17.clone.1 | convolution fusion | flops 1088946176 | bytes 11550720 | tf_op jit(solution)/shard_map/while/body/eval_jaxpr/hqk,hqe->khe/dot_general | solution.py:138
  396.4 6.3 %fusion.152 = bf16[2,1024,128]{1,2,0:T(8,128)(2,1)S(1)} fusion(bf16[2,1024,128]{1,2,0:T(8,128)(2,1)} %get-tuple-element.906, f32[2,1024,1024]{2,1,0:T(8,128)} %fusion.151, f32[2,1024]{1,0:T(2,128)S(1)} %get-tuple-element.904, pred[1024,1024]{0,1:T(8,128)(4,1)S(1)} %compare_and_fusion.6), kind=kOutput, calls=%fused_computation.10.clone.1 | convolution fusion | flops 547356672 | bytes 10493952 | tf_op jit(solution)/shard_map/while/body/eval_jaxpr/hqk,hqe->khe/dot_general | solution.py:134
  404.5 71.0 %while.39 = (s32[]{:T(128)}, f32[2,1024,128]{2,1,0:T(8,128)}, s32[4]{0:T(128)S(1)}, s32[4,1024]{1,0:T(4,128)S(1)}, s32[1024]{0:T(1024)S(1)}, /*index=5*/bf16[4,1...) while((s32[]{:T(128)}, f32[2,1024,128]{2,1,0:T(8,128)}, ...), condition=%wide.region_10.11_spmd.clone, body=%wide.region_9.10_spmd.clone.sunk | while | flops 1629227008 | bytes 27836616 | solution.py:33
  408.5 4.8 fusion.169
  413.2 9.0 %fusion.170 = f32[2,1024,128]{2,1,0:T(8,128)} fusion(bf16[1024,2,128]{0,2,1:T(8,128)(2,1)S(1)} %bitcast.223, f32[2,1024,1024]{2,1,0:T(8,128)} %fusion.169, f32[2,1024]{1,0:T(2,128)S(1)} %get-tuple-element.861, f32[2,1024]{1,0:T(2,128)S(1)} %get-tuple-element.858, pred[1024,1024]{0,1:T(8,128)(4,1)S(1)} %compare_and_fusion.8, ...), kind=kOutput, calls=%fused_computation.63.clone.1 | convolution fusion | flops 1089208320 | bytes 13123585 | tf_op jit(solution)/shard_map/while/body/eval_jaxpr/hqk,khe->hqe/dot_general | solution.py:142
  426.1 4.5 fusion.169
  430.6 9.4 %fusion.170 = f32[2,1024,128]{2,1,0:T(8,128)} fusion(bf16[1024,2,128]{0,2,1:T(8,128)(2,1)S(1)} %bitcast.223, f32[2,1024,1024]{2,1,0:T(8,128)} %fusion.169, f32[2,1024]{1,0:T(2,128)S(1)} %get-tuple-element.861, f32[2,1024]{1,0:T(2,128)S(1)} %get-tuple-element.858, pred[1024,1024]{0,1:T(8,128)(4,1)S(1)} %compare_and_fusion.8, ...), kind=kOutput, calls=%fused_computation.63.clone.1 | convolution fusion | flops 1089208320 | bytes 13123585 | tf_op jit(solution)/shard_map/while/body/eval_jaxpr/hqk,khe->hqe/dot_general | solution.py:142
  443.8 4.5 fusion.169
  448.3 9.4 %fusion.170 = f32[2,1024,128]{2,1,0:T(8,128)} fusion(bf16[1024,2,128]{0,2,1:T(8,128)(2,1)S(1)} %bitcast.223, f32[2,1024,1024]{2,1,0:T(8,128)} %fusion.169, f32[2,1024]{1,0:T(2,128)S(1)} %get-tuple-element.861, f32[2,1024]{1,0:T(2,128)S(1)} %get-tuple-element.858, pred[1024,1024]{0,1:T(8,128)(4,1)S(1)} %compare_and_fusion.8, ...), kind=kOutput, calls=%fused_computation.63.clone.1 | convolution fusion | flops 1089208320 | bytes 13123585 | tf_op jit(solution)/shard_map/while/body/eval_jaxpr/hqk,khe->hqe/dot_general | solution.py:142
  461.5 4.5 fusion.169
  466.0 9.3 %fusion.170 = f32[2,1024,128]{2,1,0:T(8,128)} fusion(bf16[1024,2,128]{0,2,1:T(8,128)(2,1)S(1)} %bitcast.223, f32[2,1024,1024]{2,1,0:T(8,128)} %fusion.169, f32[2,1024]{1,0:T(2,128)S(1)} %get-tuple-element.861, f32[2,1024]{1,0:T(2,128)S(1)} %get-tuple-element.858, pred[1024,1024]{0,1:T(8,128)(4,1)S(1)} %compare_and_fusion.8, ...), kind=kOutput, calls=%fused_computation.63.clone.1 | convolution fusion | flops 1089208320 | bytes 13123585 | tf_op jit(solution)/shard_map/while/body/eval_jaxpr/hqk,khe->hqe/dot_general | solution.py:142
  476.9 5.8 %fusion.85 = f32[1024,2048]{1,0:T(8,128)} fusion(bf16[1024,256]{0,1:T(8,128)(2,1)S(1)} %bitcast.238, bf16[3,2048,256]{2,1,0:T(8,128)(2,1)} %param.15), kind=kOutput, calls=%fused_computation.96 | convolution fusion | flops 1073741824 | bytes 9961472 | tf_op jit(solution)/shard_map/sn,dn->sd/dot_general | solution.py:182
  486.8 4.7 add_convert_fusion
  491.5 6.6 %convert_element_type.75 = f32[1024,2048]{1,0:T(8,128)} convert(bf16[1024,2048]{1,0:T(8,128)(2,1)} %param.13) | non-fusion elementwise | flops 2097152 | bytes 12582912 | tf_op jit(solution)/shard_map/convert_element_type | solution.py:45
  498.9 42.9 %reduce-scatter.5.cloned.1.call-done = bf16[128,2048]{1,0:T(8,128)(2,1)} async-done(((bf16[1024,2048]{1,0:T(8,128)(2,1)}), bf16[128,2048]{1,0:T(8,128)(2,1)}) %reduce-scatter.5.cloned.1.call-update) | async-done | bytes 524304 | tf_op jit(solution)/shard_map/reduce_scatter | solution.py:186
  (173 shorter events, 98.2 us)
Async XLA Ops:
  6.5 182.3 %copy-start = (bf16[256,2048]{1,0:T(8,128)(2,1)S(1)}, bf16[256,2048]{1,0:T(8,128)(2,1)}, u32[]{:S(2)}) copy-start(bf16[256,2048]{1,0:T(8,128)(2,1)} %param.16) | copy-start | bytes 3145732
  6.5 50.1 %all-gather.5.cloned.1.call-start = ((), (), s32[]{:S(2)}) async-start(), calls=%async_computation.5 | async-start | bytes 2621440 | tf_op jit(solution)/shard_map/all_gather | solution.py:91
  7.3 10.0 %copy-start.13 = (f32[2048]{0:T(1024)}, f32[2048]{0:T(1024)S(1)}, u32[]{:S(2)}) copy-start(f32[2048]{0:T(1024)S(1)} %convert_element_type.76) | copy-start | bytes 24580
  10.4 7.0 %copy-start.15 = (f32[1024]{0:T(1024)}, f32[1024]{0:T(1024)S(1)}, u32[]{:S(2)}) copy-start(f32[1024]{0:T(1024)S(1)} %add_rsqrt_fusion.1) | copy-start | bytes 12292
  10.4 9.2 %copy-start.10 = (s32[1024]{0:T(1024)S(1)}, s32[1024]{0:T(1024)}, u32[]{:S(2)}) copy-start(s32[1024]{0:T(1024)} %param.19) | copy-start | bytes 12292
  18.5 75.1 %all-gather.7.cloned.1.call-start = ((), (), s32[]{:S(2)}) async-start(), calls=%async_computation.6 | async-start | bytes 2621440 | tf_op jit(solution)/shard_map/all_gather | solution.py:92
  19.3 269.4 %all-reduce.2.cloned.1.call-start = ((), (), s32[]{:S(2)}) async-start(), calls=%async_computation.2 | async-start | bytes 8388608 | tf_op jit(solution)/shard_map/psum | solution.py:104
  111.5 5.8 %copy-start.2 = (f32[2,1024,1024]{2,1,0:T(8,128)S(1)}, f32[2,1024,1024]{2,1,0:T(8,128)}, u32[]{:S(2)}) copy-start(f32[2,1024,1024]{2,1,0:T(8,128)} %get-tuple-element.764) | copy-start | bytes 25165828 | tf_op jit(solution)/shard_map/while
  111.5 5.9 %copy-start.8 = (bf16[1,1024,256]{1,2,0:T(8,128)(2,1)S(1)}, bf16[1,1024,256]{1,2,0:T(8,128)(2,1)}, u32[]{:S(2)}) copy-start(bf16[1,1024,256]{1,2,0:T(8,128)(2,1)} %get-tuple-element.766) | copy-start | bytes 1572868 | tf_op jit(solution)/shard_map/while
  131.5 5.8 %copy-start.2 = (f32[2,1024,1024]{2,1,0:T(8,128)S(1)}, f32[2,1024,1024]{2,1,0:T(8,128)}, u32[]{:S(2)}) copy-start(f32[2,1024,1024]{2,1,0:T(8,128)} %get-tuple-element.764) | copy-start | bytes 25165828 | tf_op jit(solution)/shard_map/while
  131.5 5.9 %copy-start.8 = (bf16[1,1024,256]{1,2,0:T(8,128)(2,1)S(1)}, bf16[1,1024,256]{1,2,0:T(8,128)(2,1)}, u32[]{:S(2)}) copy-start(bf16[1,1024,256]{1,2,0:T(8,128)(2,1)} %get-tuple-element.766) | copy-start | bytes 1572868 | tf_op jit(solution)/shard_map/while
  152.6 5.8 %copy-start.2 = (f32[2,1024,1024]{2,1,0:T(8,128)S(1)}, f32[2,1024,1024]{2,1,0:T(8,128)}, u32[]{:S(2)}) copy-start(f32[2,1024,1024]{2,1,0:T(8,128)} %get-tuple-element.764) | copy-start | bytes 25165828 | tf_op jit(solution)/shard_map/while
  152.6 5.9 %copy-start.8 = (bf16[1,1024,256]{1,2,0:T(8,128)(2,1)S(1)}, bf16[1,1024,256]{1,2,0:T(8,128)(2,1)}, u32[]{:S(2)}) copy-start(bf16[1,1024,256]{1,2,0:T(8,128)(2,1)} %get-tuple-element.766) | copy-start | bytes 1572868 | tf_op jit(solution)/shard_map/while
  173.6 5.8 %copy-start.2 = (f32[2,1024,1024]{2,1,0:T(8,128)S(1)}, f32[2,1024,1024]{2,1,0:T(8,128)}, u32[]{:S(2)}) copy-start(f32[2,1024,1024]{2,1,0:T(8,128)} %get-tuple-element.764) | copy-start | bytes 25165828 | tf_op jit(solution)/shard_map/while
  173.6 5.9 %copy-start.8 = (bf16[1,1024,256]{1,2,0:T(8,128)(2,1)S(1)}, bf16[1,1024,256]{1,2,0:T(8,128)(2,1)}, u32[]{:S(2)}) copy-start(bf16[1,1024,256]{1,2,0:T(8,128)(2,1)} %get-tuple-element.766) | copy-start | bytes 1572868 | tf_op jit(solution)/shard_map/while
  192.1 290.6 %reduce-scatter.3.cloned.1.call-start = ((), (), s32[]{:S(2)}) async-start(), calls=%async_computation.3 | async-start | bytes 5242880 | tf_op jit(solution)/shard_map/reduce_scatter | solution.py:167
  288.7 6.0 %copy-start.3 = (bf16[1024,2048]{1,0:T(8,128)(2,1)S(1)}, bf16[1024,2048]{1,0:T(8,128)(2,1)}, u32[]{:S(2)}) copy-start(bf16[1024,2048]{1,0:T(8,128)(2,1)} %param.13) | copy-start | bytes 12582916
  288.7 7.1 %copy-start.6 = (bf16[1024,2048]{1,0:T(8,128)(2,1)S(1)}, bf16[1024,2048]{1,0:T(8,128)(2,1)}, u32[]{:S(2)}) copy-start(bf16[1024,2048]{1,0:T(8,128)(2,1)} %param.17) | copy-start | bytes 12582916
  288.7 8.3 %copy-start.7 = (bf16[1024,2048]{1,0:T(8,128)(2,1)S(1)}, bf16[1024,2048]{1,0:T(8,128)(2,1)}, u32[]{:S(2)}) copy-start(bf16[1024,2048]{1,0:T(8,128)(2,1)} %all-reduce.2.cloned.1.call-done) | copy-start | bytes 12582916
  299.6 3.2 copy-start.5
  404.4 137.4 %reduce-scatter.5.cloned.1.call-start = ((), (), s32[]{:S(2)}) async-start(), calls=%async_computation.4 | async-start | bytes 4718592 | tf_op jit(solution)/shard_map/reduce_scatter | solution.py:186
  404.7 8.6 %copy-start.11 = (bf16[2,1024,128]{2,1,0:T(8,128)(2,1)S(1)}, bf16[2,1024,128]{2,1,0:T(8,128)(2,1)}, u32[]{:S(2)}) copy-start(bf16[2,1024,128]{2,1,0:T(8,128)(2,1)} %get-tuple-element.860) | copy-start | bytes 1572868 | tf_op jit(solution)/shard_map/while
  422.3 8.3 %copy-start.11 = (bf16[2,1024,128]{2,1,0:T(8,128)(2,1)S(1)}, bf16[2,1024,128]{2,1,0:T(8,128)(2,1)}, u32[]{:S(2)}) copy-start(bf16[2,1024,128]{2,1,0:T(8,128)(2,1)} %get-tuple-element.860) | copy-start | bytes 1572868 | tf_op jit(solution)/shard_map/while
  440.0 8.4 %copy-start.11 = (bf16[2,1024,128]{2,1,0:T(8,128)(2,1)S(1)}, bf16[2,1024,128]{2,1,0:T(8,128)(2,1)}, u32[]{:S(2)}) copy-start(bf16[2,1024,128]{2,1,0:T(8,128)(2,1)} %get-tuple-element.860) | copy-start | bytes 1572868 | tf_op jit(solution)/shard_map/while
  457.7 8.3 %copy-start.11 = (bf16[2,1024,128]{2,1,0:T(8,128)(2,1)S(1)}, bf16[2,1024,128]{2,1,0:T(8,128)(2,1)}, u32[]{:S(2)}) copy-start(bf16[2,1024,128]{2,1,0:T(8,128)(2,1)} %get-tuple-element.860) | copy-start | bytes 1572868 | tf_op jit(solution)/shard_map/while
  482.7 3.9 copy-start.4
  482.7 4.1 copy-start.9
  491.5 50.4 %copy-start.14 = (f32[2048]{0:T(1024)S(1)}, f32[2048]{0:T(1024)}, u32[]{:S(2)}) copy-start(f32[2048]{0:T(1024)} %copy-done.13) | copy-start | bytes 24580
  491.5 52.0 %copy-start.12 = (bf16[128,2048]{1,0:T(8,128)(2,1)S(1)}, bf16[128,2048]{1,0:T(8,128)(2,1)}, u32[]{:S(2)}) copy-start(bf16[128,2048]{1,0:T(8,128)(2,1)} %param.18) | copy-start | bytes 1572868
  491.5 55.1 %copy-start.1 = (bf16[256,2048]{1,0:T(8,128)(2,1)S(1)}, bf16[256,2048]{1,0:T(8,128)(2,1)}, u32[]{:S(2)}) copy-start(bf16[256,2048]{1,0:T(8,128)(2,1)} %param.16) | copy-start | bytes 3145732
Sparse Core Ops, SparseCore 0:
  18.6 37.8 all-gather.4
  58.4 35.1 all-gather.6
  192.2 96.4 all-reduce.1
  404.6 52.6 reduce-scatter.2
  491.6 50.1 reduce-scatter.4
where the time goes:
time: 559 us; the launch traced here: 553 us
  matrix products  198 us (35%)
  waiting for transfers between devices  196 us (35%)
  local copies, waits for them, and re-layouts  67.8 us (12%)
  other arithmetic  64.9 us (12%)
  between operations  13.6 us (2%)
  blocking collectives  9.97 us (2%)
    psum x1, waiting for transfers between devices, body(): lax.psum(term.astype(jnp.bfloat16), 'head').astype(jnp.float32)  96 us
    reduce_scatter x1, waiting for transfers between devices, body(): lax.psum_scatter((running + jnp.einsum('sn,dn->sd', value_grad, w_qkv[2],...  42.9 us
    dot_general x4, matrix products, back_block(): jnp.einsum('hqk,khe->hqe', dscore_half, key_heads, preferred_element_type...  37.1 us
    dot_general x8, matrix products, back_block(): jnp.einsum('hqe,khe->hqk', queries, key_heads, preferred_element_type=jnp...  36.6 us
    dot_general x4, matrix products, back_block(): jnp.einsum('hqk,hqe->khe', dscore_half, queries, preferred_element_type=j...  32 us
    all_gather x1, waiting for transfers between devices, body(): lax.all_gather(value_rows, 'ctx', axis=0, tiled=True)  28.9 us
    all_gather x1, waiting for transfers between devices, body(): lax.all_gather(key_rows, 'ctx', axis=0, tiled=True)  26.9 us
    dot_general x4, matrix products, back_block(): jnp.einsum('hqk,hqe->khe', prob_half, grads_out, preferred_element_type=j...  25.3 us
  transfers between devices with their start and end apart: 5, of which 4 were waited for; matrix products, arithmetic and copies ran while one was open for 17% of the time, Pallas kernels for 0%

commit v1 on v0

--- a/solution.py
+++ b/solution.py
@@ -1,3 +1,4 @@
+import functools
 import jax
 import jax.numpy as jnp
 from jax import lax
@@ -7,6 +8,36 @@
 EPSILON = 1e-05
 STEP_SIZE = 0.25
 NEGATIVE = -1e30
+
+
+def advance_orders_in(sample, array_axis):
+    sample = jnp.moveaxis(sample, 0, array_axis)
+    t_next = sample.shape
+    return sample.reshape(
+        *t_next[:array_axis], t_next[array_axis] * t_next[array_axis + 1], *t_next[array_axis + 2 :]
+    )
+
+
+def press_the_kinds(m, mesh_name):
+    n_now, m_next = (lax.axis_size(mesh_name), lax.axis_index(mesh_name))
+    part_next, wide_out = (m[None], 1)
+    while wide_out < n_now:
+        h_now = lax.ppermute(
+            part_next, axis_name=mesh_name, perm=[(dev, dev ^ wide_out) for dev in range(n_now)]
+        )
+        shaped = m_next & wide_out == 0
+        part_next = jnp.concatenate(
+            [jnp.where(shaped, part_next, h_now), jnp.where(shaped, h_now, part_next)]
+        )
+        wide_out *= 2
+    return part_next
+
+
+def spots_see(xs, tile_in, on_dim):
+    return advance_orders_in(press_the_kinds(xs, tile_in), on_dim)
+
+
+mix_knots = functools.partial(spots_see, tile_in="ctx", on_dim=0)
 
 
 def row_scale(matrix):
@@ -89,7 +120,7 @@
     )
     all_keys, all_values, all_segs = (
         lax.all_gather(key_rows, "ctx", axis=0, tiled=True),
-        lax.all_gather(value_rows, "ctx", axis=0, tiled=True),
+        mix_knots(value_rows),
         lax.all_gather(segment_ids, "ctx", axis=0, tiled=True),
     )
     run_max, run_sum, run_acc = over_blocks(

time: 559 us -> 542 us (0.970)
  waiting for transfers between devices: 196 us -> 152 us
  blocking collectives: 9.97 us -> 33.3 us
  local copies, waits for them, and re-layouts: 67.8 us -> 61.7 us
    all_gather x1 -> x0, waiting for transfers between devices: 28.9 us -> none  [body(): lax.all_gather(value_rows, 'ctx', axis=0, tiled=True)]
    all_gather x1, waiting for transfers between devices: 26.9 us -> 1.22 us  [body(): lax.all_gather(key_rows, 'ctx', axis=0, tiled=True)]
    all_gather x1, blocking collectives: 9.97 us -> 33.3 us  [body(): lax.all_gather(segment_ids, 'ctx', axis=0, tiled=True)]
    ppermute x0 -> x2, waiting for transfers between devices: none -> 11.9 us  [press_the_kinds(): lax.ppermute(part_next, axis_name=mesh_name, perm=[(dev, dev ^ wide_out)...]
    reshape x3 -> x1, local copies, waits for them, and re-layouts: 9.06 us -> 0.01 us  [over_blocks(): member.reshape((number, block_size) + member.shape[1:])]
    dot_general x4, matrix products: 20.6 us -> 15 us  [forward_block(): jnp.einsum('hqk,khe->hqe', weights.astype(jnp.bfloat16), value_heads, pre...]
    unnamed x29 -> x39, local copies, waits for them, and re-layouts: 16.1 us -> 16.8 us
  transfers between devices with their start and end apart: 5 -> 6, of which waited for: 4 -> 4; matrix products, arithmetic and copies ran while one was open for 17% -> 17% of each run, Pallas kernels for 0% -> 0%
where the time goes in v1:
time: 542 us; the launch traced here: 538 us
  matrix products  200 us (37%)
  waiting for transfers between devices  152 us (28%)
  other arithmetic  68 us (13%)
  local copies, waits for them, and re-layouts  61.7 us (11%)
  blocking collectives  33.3 us (6%)
  between operations  13.6 us (3%)
  starting transfers between devices  5.46 us (1%)
    psum x1, waiting for transfers between devices, body(): lax.psum(term.astype(jnp.bfloat16), 'head').astype(jnp.float32)  96.1 us
    reduce_scatter x1, waiting for transfers between devices, body(): lax.psum_scatter((running + jnp.einsum('sn,dn->sd', value_grad, w_qkv[2],...  43 us
    dot_general x8, matrix products, back_block(): jnp.einsum('hqe,khe->hqk', queries, key_heads, preferred_element_type=jnp...  40.8 us
    dot_general x4, matrix products, back_block(): jnp.einsum('hqk,khe->hqe', dscore_half, key_heads, preferred_element_type...  37.1 us
    all_gather x1, blocking collectives, body(): lax.all_gather(segment_ids, 'ctx', axis=0, tiled=True)  33.3 us
    dot_general x4, matrix products, back_block(): jnp.einsum('hqk,hqe->khe', dscore_half, queries, preferred_element_type=j...  32 us
    dot_general x4, matrix products, back_block(): jnp.einsum('hqk,hqe->khe', prob_half, grads_out, preferred_element_type=j...  25.4 us
    dot_general x4, matrix products, forward_block(): jnp.einsum('hqe,khe->hqk', queries, key_heads, preferred_element_type=jnp...  24.5 us
  transfers between devices with their start and end apart: 6, of which 4 were waited for; matrix products, arithmetic and copies ran while one was open for 17% of the time, Pallas kernels for 0%

profile of v1, /device:TPU:0, one launch (start us, length us, event | category | flops | bytes accessed | tf_op | source)
XLA Modules:
  0.0 537.8 jit_solution(16273113732715565183)
XLA Ops:
  10.4 6.6 %fusion.73 = bf16[3,1024,256]{2,1,0:T(8,128)(2,1)S(1)} fusion(bf16[3,2048,256]{2,1,0:T(8,128)(2,1)} %param.15, bf16[1024,2048]{1,0:T(8,128)(2,1)} %param.13, f32[2048]{0:T(1024)S(1)} %convert_element_type.76, f32[1024]{0:T(1024)S(1)} %add_rsqrt_fusion.1), kind=kOutput, calls=%fused_computation.91 | convolution fusion | flops 3230400512 | bytes 8925184 | tf_op jit(solution)/shard_map/sd,cdn->csn/dot_general | solution.py:80
  21.3 11.9 %collective-permute-done = bf16[1,1024,256]{2,1,0:T(8,128)(2,1)S(1)} collective-permute-done((bf16[1,1024,256]{2,1,0:T(8,128)(2,1)S(1)}, bf16[1,1024,256]{2,1,0:T(8,128)(2,1)S(1)}, u32[]{:S(2)}, u32[]{:S(2)}) %collective-permute-start) | collective-permute-done | bytes 524320 | tf_op jit(solution)/shard_map/ppermute | solution.py:25
  38.5 33.3 %all_gather.6 = s32[4096]{0:T(1024)S(1)} all-gather(s32[1024]{0:T(1024)S(1)} %copy-done.15), channel_id=1, replica_groups=mesh['ctx'=4,'head'=8] {'ctx'}, dimensions={0}, use_global_device_ids=true | all-gather | bytes 20480 | tf_op jit(solution)/shard_map/all_gather | solution.py:124
  78.5 4.0 copy.69
  82.5 82.1 %while.38 = (s32[]{:T(128)}, f32[2,1024]{1,0:T(2,128)S(1)}, f32[2,1024]{1,0:T(2,128)S(1)}, f32[2,1024,128]{2,1,0:T(8,128)}, s32[4]{0:T(128)S(1)}, /*index=5*/s32...) while((s32[]{:T(128)}, f32[2,1024]{1,0:T(2,128)S(1)}, ...), condition=%wide.region_4.5_spmd.clone, body=%wide.region_1.4_spmd.clone.sunk | while | flops 1104949248 | bytes 77234424 | solution.py:64
  86.1 6.1 %fusion.157 = (f32[2,1024]{1,0:T(2,128)S(1)}, f32[2,1024,1024]{2,1,0:T(8,128)}) fusion(pred[1024,1024]{0,1:T(8,128)(4,1)S(1)} %compare_and_fusion.7, bf16[1024,2,128]{0,2,1:T(8,128)(2,1)S(1)} %bitcast.227, bf16[2,1024,128]{2,1,0:T(8,128)(2,1)} %get-tuple-element.810), kind=kOutput, calls=%fused_computation.31.clone.1 | convolution fusion | flops 543160320 | bytes 10493952 | tf_op jit(solution)/shard_map/while/body/eval_jaxpr/hqe,khe->hqk/dot_general | solution.py:100
  92.2 4.7 fusion.159
  98.3 3.7 fusion.161
  106.6 6.1 %fusion.157 = (f32[2,1024]{1,0:T(2,128)S(1)}, f32[2,1024,1024]{2,1,0:T(8,128)}) fusion(pred[1024,1024]{0,1:T(8,128)(4,1)S(1)} %compare_and_fusion.7, bf16[1024,2,128]{0,2,1:T(8,128)(2,1)S(1)} %bitcast.227, bf16[2,1024,128]{2,1,0:T(8,128)(2,1)} %get-tuple-element.810), kind=kOutput, calls=%fused_computation.31.clone.1 | convolution fusion | flops 543160320 | bytes 10493952 | tf_op jit(solution)/shard_map/while/body/eval_jaxpr/hqe,khe->hqk/dot_general | solution.py:100
  112.8 4.7 fusion.159
  118.8 3.7 fusion.161
  127.1 6.1 %fusion.157 = (f32[2,1024]{1,0:T(2,128)S(1)}, f32[2,1024,1024]{2,1,0:T(8,128)}) fusion(pred[1024,1024]{0,1:T(8,128)(4,1)S(1)} %compare_and_fusion.7, bf16[1024,2,128]{0,2,1:T(8,128)(2,1)S(1)} %bitcast.227, bf16[2,1024,128]{2,1,0:T(8,128)(2,1)} %get-tuple-element.810), kind=kOutput, calls=%fused_computation.31.clone.1 | convolution fusion | flops 543160320 | bytes 10493952 | tf_op jit(solution)/shard_map/while/body/eval_jaxpr/hqe,khe->hqk/dot_general | solution.py:100
  133.3 4.7 fusion.159
  139.3 3.7 fusion.161
  147.7 6.1 %fusion.157 = (f32[2,1024]{1,0:T(2,128)S(1)}, f32[2,1024,1024]{2,1,0:T(8,128)}) fusion(pred[1024,1024]{0,1:T(8,128)(4,1)S(1)} %compare_and_fusion.7, bf16[1024,2,128]{0,2,1:T(8,128)(2,1)S(1)} %bitcast.227, bf16[2,1024,128]{2,1,0:T(8,128)(2,1)} %get-tuple-element.810), kind=kOutput, calls=%fused_computation.31.clone.1 | convolution fusion | flops 543160320 | bytes 10493952 | tf_op jit(solution)/shard_map/while/body/eval_jaxpr/hqe,khe->hqk/dot_general | solution.py:100
  153.8 4.7 fusion.159
  159.9 3.7 fusion.161
  166.3 3.3 convolution_convert_fusion
  171.4 96.1 %all-reduce.2.cloned.1.call-done = bf16[1024,2048]{1,0:T(8,128)(2,1)} async-done(((bf16[1024,2048]{1,0:T(8,128)(2,1)}), bf16[1024,2048]{1,0:T(8,128)(2,1)}) %all-reduce.2.cloned.1.call-update) | async-done | bytes 4194320 | tf_op jit(solution)/shard_map/psum | solution.py:135
  267.5 6.0 %multiply_reduce_fusion = (f32[1024]{0:T(1024)S(1)}, f32[1024]{0:T(1024)S(1)}) fusion(bf16[1024,2048]{1,0:T(8,128)(2,1)} %all-reduce.2.cloned.1.call-done, bf16[1024,2048]{1,0:T(8,128)(2,1)} %param.13, bf16[1024,2048]{1,0:T(8,128)(2,1)} %param.17), kind=kLoop, calls=%fused_computation.77 | loop fusion | flops 16775168 | bytes 12591104 | tf_op jit(solution)/shard_map/reduce_sum | solution.py:44
  278.4 3.2 copy-done.5
  285.9 103.1 %while.37 = (s32[]{:T(128)}, bf16[4,1024,512]{2,1,0:T(8,128)(2,1)}, s32[4]{0:T(128)S(1)}, s32[4096]{0:T(1024)S(1)}, s32[1024]{0:T(1024)S(1)}, /*index=5*/bf16[40...) while((s32[]{:T(128)}, bf16[4,1024,512]{2,1,0:T(8,128)(2,1)}, ...), condition=%wide.region_12.13_spmd.clone, body=%wide.region_11.12_spmd.clone.sunk | while | flops 2178418688 | bytes 45146872 | solution.py:197
  289.8 5.6 %fusion.150 = f32[2,1024,1024]{2,1,0:T(8,128)} fusion(bf16[1024,2,128]{0,2,1:T(8,128)(2,1)S(1)} %bitcast.221, bf16[2,1024,128]{1,2,0:T(8,128)(2,1)} %get-tuple-element.895), kind=kOutput, calls=%fused_computation.124.clone.1 | convolution fusion | flops 536870912 | bytes 9437184 | tf_op jit(solution)/shard_map/while/body/eval_jaxpr/hqe,khe->hqk/dot_general | solution.py:153
  295.6 8.0 %fusion.152 = bf16[2,1024,128]{1,2,0:T(8,128)(2,1)S(1)} fusion(bf16[2,1024,128]{1,2,0:T(8,128)(2,1)S(1)} %copy-done.8, f32[2,1024,1024]{2,1,0:T(8,128)} %fusion.150, f32[2,1024]{1,0:T(2,128)S(1)} %get-tuple-element.899, f32[2,1024]{1,0:T(2,128)S(1)} %get-tuple-element.896, pred[1024,1024]{0,1:T(8,128)(4,1)S(1)} %compare_and_fusion.6, ...), kind=kOutput, calls=%fused_computation.17.clone.1 | convolution fusion | flops 1088946176 | bytes 11550720 | tf_op jit(solution)/shard_map/while/body/eval_jaxpr/hqk,hqe->khe/dot_general | solution.py:169
  303.6 6.3 %fusion.151 = bf16[2,1024,128]{1,2,0:T(8,128)(2,1)S(1)} fusion(bf16[2,1024,128]{1,2,0:T(8,128)(2,1)} %get-tuple-element.898, f32[2,1024,1024]{2,1,0:T(8,128)} %fusion.150, f32[2,1024]{1,0:T(2,128)S(1)} %get-tuple-element.896, pred[1024,1024]{0,1:T(8,128)(4,1)S(1)} %compare_and_fusion.6), kind=kOutput, calls=%fused_computation.10.clone.1 | convolution fusion | flops 547356672 | bytes 10493952 | tf_op jit(solution)/shard_map/while/body/eval_jaxpr/hqk,hqe->khe/dot_general | solution.py:165
  315.5 5.6 %fusion.150 = f32[2,1024,1024]{2,1,0:T(8,128)} fusion(bf16[1024,2,128]{0,2,1:T(8,128)(2,1)S(1)} %bitcast.221, bf16[2,1024,128]{1,2,0:T(8,128)(2,1)} %get-tuple-element.895), kind=kOutput, calls=%fused_computation.124.clone.1 | convolution fusion | flops 536870912 | bytes 9437184 | tf_op jit(solution)/shard_map/while/body/eval_jaxpr/hqe,khe->hqk/dot_general | solution.py:153
  321.4 8.0 %fusion.152 = bf16[2,1024,128]{1,2,0:T(8,128)(2,1)S(1)} fusion(bf16[2,1024,128]{1,2,0:T(8,128)(2,1)S(1)} %copy-done.8, f32[2,1024,1024]{2,1,0:T(8,128)} %fusion.150, f32[2,1024]{1,0:T(2,128)S(1)} %get-tuple-element.899, f32[2,1024]{1,0:T(2,128)S(1)} %get-tuple-element.896, pred[1024,1024]{0,1:T(8,128)(4,1)S(1)} %compare_and_fusion.6, ...), kind=kOutput, calls=%fused_computation.17.clone.1 | convolution fusion | flops 1088946176 | bytes 11550720 | tf_op jit(solution)/shard_map/while/body/eval_jaxpr/hqk,hqe->khe/dot_general | solution.py:169
  329.4 6.3 %fusion.151 = bf16[2,1024,128]{1,2,0:T(8,128)(2,1)S(1)} fusion(bf16[2,1024,128]{1,2,0:T(8,128)(2,1)} %get-tuple-element.898, f32[2,1024,1024]{2,1,0:T(8,128)} %fusion.150, f32[2,1024]{1,0:T(2,128)S(1)} %get-tuple-element.896, pred[1024,1024]{0,1:T(8,128)(4,1)S(1)} %compare_and_fusion.6), kind=kOutput, calls=%fused_computation.10.clone.1 | convolution fusion | flops 547356672 | bytes 10493952 | tf_op jit(solution)/shard_map/while/body/eval_jaxpr/hqk,hqe->khe/dot_general | solution.py:165
  341.3 5.6 %fusion.150 = f32[2,1024,1024]{2,1,0:T(8,128)} fusion(bf16[1024,2,128]{0,2,1:T(8,128)(2,1)S(1)} %bitcast.221, bf16[2,1024,128]{1,2,0:T(8,128)(2,1)} %get-tuple-element.895), kind=kOutput, calls=%fused_computation.124.clone.1 | convolution fusion | flops 536870912 | bytes 9437184 | tf_op jit(solution)/shard_map/while/body/eval_jaxpr/hqe,khe->hqk/dot_general | solution.py:153
  347.1 8.0 %fusion.152 = bf16[2,1024,128]{1,2,0:T(8,128)(2,1)S(1)} fusion(bf16[2,1024,128]{1,2,0:T(8,128)(2,1)S(1)} %copy-done.8, f32[2,1024,1024]{2,1,0:T(8,128)} %fusion.150, f32[2,1024]{1,0:T(2,128)S(1)} %get-tuple-element.899, f32[2,1024]{1,0:T(2,128)S(1)} %get-tuple-element.896, pred[1024,1024]{0,1:T(8,128)(4,1)S(1)} %compare_and_fusion.6, ...), kind=kOutput, calls=%fused_computation.17.clone.1 | convolution fusion | flops 1088946176 | bytes 11550720 | tf_op jit(solution)/shard_map/while/body/eval_jaxpr/hqk,hqe->khe/dot_general | solution.py:169
  355.1 6.3 %fusion.151 = bf16[2,1024,128]{1,2,0:T(8,128)(2,1)S(1)} fusion(bf16[2,1024,128]{1,2,0:T(8,128)(2,1)} %get-tuple-element.898, f32[2,1024,1024]{2,1,0:T(8,128)} %fusion.150, f32[2,1024]{1,0:T(2,128)S(1)} %get-tuple-element.896, pred[1024,1024]{0,1:T(8,128)(4,1)S(1)} %compare_and_fusion.6), kind=kOutput, calls=%fused_computation.10.clone.1 | convolution fusion | flops 547356672 | bytes 10493952 | tf_op jit(solution)/shard_map/while/body/eval_jaxpr/hqk,hqe->khe/dot_general | solution.py:165
  367.1 5.6 %fusion.150 = f32[2,1024,1024]{2,1,0:T(8,128)} fusion(bf16[1024,2,128]{0,2,1:T(8,128)(2,1)S(1)} %bitcast.221, bf16[2,1024,128]{1,2,0:T(8,128)(2,1)} %get-tuple-element.895), kind=kOutput, calls=%fused_computation.124.clone.1 | convolution fusion | flops 536870912 | bytes 9437184 | tf_op jit(solution)/shard_map/while/body/eval_jaxpr/hqe,khe->hqk/dot_general | solution.py:153
  372.9 8.0 %fusion.152 = bf16[2,1024,128]{1,2,0:T(8,128)(2,1)S(1)} fusion(bf16[2,1024,128]{1,2,0:T(8,128)(2,1)S(1)} %copy-done.8, f32[2,1024,1024]{2,1,0:T(8,128)} %fusion.150, f32[2,1024]{1,0:T(2,128)S(1)} %get-tuple-element.899, f32[2,1024]{1,0:T(2,128)S(1)} %get-tuple-element.896, pred[1024,1024]{0,1:T(8,128)(4,1)S(1)} %compare_and_fusion.6, ...), kind=kOutput, calls=%fused_computation.17.clone.1 | convolution fusion | flops 1088946176 | bytes 11550720 | tf_op jit(solution)/shard_map/while/body/eval_jaxpr/hqk,hqe->khe/dot_general | solution.py:169
  380.9 6.3 %fusion.151 = bf16[2,1024,128]{1,2,0:T(8,128)(2,1)S(1)} fusion(bf16[2,1024,128]{1,2,0:T(8,128)(2,1)} %get-tuple-element.898, f32[2,1024,1024]{2,1,0:T(8,128)} %fusion.150, f32[2,1024]{1,0:T(2,128)S(1)} %get-tuple-element.896, pred[1024,1024]{0,1:T(8,128)(4,1)S(1)} %compare_and_fusion.6), kind=kOutput, calls=%fused_computation.10.clone.1 | convolution fusion | flops 547356672 | bytes 10493952 | tf_op jit(solution)/shard_map/while/body/eval_jaxpr/hqk,hqe->khe/dot_general | solution.py:165
  389.0 70.9 %while.39 = (s32[]{:T(128)}, f32[2,1024,128]{2,1,0:T(8,128)}, s32[4]{0:T(128)S(1)}, s32[4,1024]{1,0:T(4,128)S(1)}, s32[1024]{0:T(1024)S(1)}, /*index=5*/bf16[4,1...) while((s32[]{:T(128)}, f32[2,1024,128]{2,1,0:T(8,128)}, ...), condition=%wide.region_10.11_spmd.clone, body=%wide.region_9.10_spmd.clone.sunk | while | flops 1629227008 | bytes 27836616 | solution.py:64
  393.0 4.8 fusion.168
  397.8 9.0 %fusion.169 = f32[2,1024,128]{2,1,0:T(8,128)} fusion(bf16[1024,2,128]{0,2,1:T(8,128)(2,1)S(1)} %bitcast.220, f32[2,1024,1024]{2,1,0:T(8,128)} %fusion.168, f32[2,1024]{1,0:T(2,128)S(1)} %get-tuple-element.853, f32[2,1024]{1,0:T(2,128)S(1)} %get-tuple-element.850, pred[1024,1024]{0,1:T(8,128)(4,1)S(1)} %compare_and_fusion.8, ...), kind=kOutput, calls=%fused_computation.63.clone.1 | convolution fusion | flops 1089208320 | bytes 13123585 | tf_op jit(solution)/shard_map/while/body/eval_jaxpr/hqk,khe->hqe/dot_general | solution.py:173
  410.6 4.5 fusion.168
  415.1 9.4 %fusion.169 = f32[2,1024,128]{2,1,0:T(8,128)} fusion(bf16[1024,2,128]{0,2,1:T(8,128)(2,1)S(1)} %bitcast.220, f32[2,1024,1024]{2,1,0:T(8,128)} %fusion.168, f32[2,1024]{1,0:T(2,128)S(1)} %get-tuple-element.853, f32[2,1024]{1,0:T(2,128)S(1)} %get-tuple-element.850, pred[1024,1024]{0,1:T(8,128)(4,1)S(1)} %compare_and_fusion.8, ...), kind=kOutput, calls=%fused_computation.63.clone.1 | convolution fusion | flops 1089208320 | bytes 13123585 | tf_op jit(solution)/shard_map/while/body/eval_jaxpr/hqk,khe->hqe/dot_general | solution.py:173
  428.3 4.5 fusion.168
  432.8 9.4 %fusion.169 = f32[2,1024,128]{2,1,0:T(8,128)} fusion(bf16[1024,2,128]{0,2,1:T(8,128)(2,1)S(1)} %bitcast.220, f32[2,1024,1024]{2,1,0:T(8,128)} %fusion.168, f32[2,1024]{1,0:T(2,128)S(1)} %get-tuple-element.853, f32[2,1024]{1,0:T(2,128)S(1)} %get-tuple-element.850, pred[1024,1024]{0,1:T(8,128)(4,1)S(1)} %compare_and_fusion.8, ...), kind=kOutput, calls=%fused_computation.63.clone.1 | convolution fusion | flops 1089208320 | bytes 13123585 | tf_op jit(solution)/shard_map/while/body/eval_jaxpr/hqk,khe->hqe/dot_general | solution.py:173
  445.9 4.5 fusion.168
  450.5 9.3 %fusion.169 = f32[2,1024,128]{2,1,0:T(8,128)} fusion(bf16[1024,2,128]{0,2,1:T(8,128)(2,1)S(1)} %bitcast.220, f32[2,1024,1024]{2,1,0:T(8,128)} %fusion.168, f32[2,1024]{1,0:T(2,128)S(1)} %get-tuple-element.853, f32[2,1024]{1,0:T(2,128)S(1)} %get-tuple-element.850, pred[1024,1024]{0,1:T(8,128)(4,1)S(1)} %compare_and_fusion.8, ...), kind=kOutput, calls=%fused_computation.63.clone.1 | convolution fusion | flops 1089208320 | bytes 13123585 | tf_op jit(solution)/shard_map/while/body/eval_jaxpr/hqk,khe->hqe/dot_general | solution.py:173
  461.4 5.8 %fusion.85 = f32[1024,2048]{1,0:T(8,128)} fusion(bf16[1024,256]{0,1:T(8,128)(2,1)S(1)} %bitcast.235, bf16[3,2048,256]{2,1,0:T(8,128)(2,1)} %param.15), kind=kOutput, calls=%fused_computation.98 | convolution fusion | flops 1073741824 | bytes 9961472 | tf_op jit(solution)/shard_map/sn,dn->sd/dot_general | solution.py:213
  471.2 4.7 add_convert_fusion
  475.9 6.6 %convert_element_type.75 = f32[1024,2048]{1,0:T(8,128)} convert(bf16[1024,2048]{1,0:T(8,128)(2,1)} %param.13) | non-fusion elementwise | flops 2097152 | bytes 12582912 | tf_op jit(solution)/shard_map/convert_element_type | solution.py:76
  483.3 43.0 %reduce-scatter.5.cloned.1.call-done = bf16[128,2048]{1,0:T(8,128)(2,1)} async-done(((bf16[1024,2048]{1,0:T(8,128)(2,1)}), bf16[128,2048]{1,0:T(8,128)(2,1)}) %reduce-scatter.5.cloned.1.call-update) | async-done | bytes 524304 | tf_op jit(solution)/shard_map/reduce_scatter | solution.py:217
  527.9 3.2 multiply_add_fusion
  (212 shorter events, 99.6 us)
Async XLA Ops:
  6.5 159.8 %copy-start = (bf16[256,2048]{1,0:T(8,128)(2,1)S(1)}, bf16[256,2048]{1,0:T(8,128)(2,1)}, u32[]{:S(2)}) copy-start(bf16[256,2048]{1,0:T(8,128)(2,1)} %param.16) | copy-start | bytes 3145732
  6.5 71.9 %all-gather.3.cloned.1.call-start = ((), (), s32[]{:S(2)}) async-start(), calls=%async_computation.5 | async-start | bytes 2621440 | tf_op jit(solution)/shard_map/all_gather | solution.py:122
  7.3 9.8 %copy-start.20 = (f32[2048]{0:T(1024)}, f32[2048]{0:T(1024)S(1)}, u32[]{:S(2)}) copy-start(f32[2048]{0:T(1024)S(1)} %convert_element_type.76) | copy-start | bytes 24580
  10.4 6.7 %copy-start.22 = (f32[1024]{0:T(1024)}, f32[1024]{0:T(1024)S(1)}, u32[]{:S(2)}) copy-start(f32[1024]{0:T(1024)S(1)} %add_rsqrt_fusion.1) | copy-start | bytes 12292
  10.4 28.1 %copy-start.15 = (s32[1024]{0:T(1024)S(1)}, s32[1024]{0:T(1024)}, u32[]{:S(2)}) copy-start(s32[1024]{0:T(1024)} %param.19) | copy-start | bytes 12292
  17.1 1.2 copy-start.13
  18.3 15.0 %collective-permute-start = (bf16[1,1024,256]{2,1,0:T(8,128)(2,1)S(1)}, bf16[1,1024,256]{2,1,0:T(8,128)(2,1)S(1)}, u32[]{:S(2)}, u32[]{:S(2)}) collective-permute-start(bf16[1,1024,256]{2,1,0:T(8,128)(2,1)S(1)} %slice.36), channel_id=1, source_target_pairs={{0,8},{8,0},{16,24},{24,16},{1,9},{9,1},{17,25},{25,17},{2,10},{10... | collective-permute-start | bytes 1572872 | tf_op jit(solution)/shard_map/ppermute | solution.py:25
  35.6 231.9 %all-reduce.2.cloned.1.call-start = ((), (), s32[]{:S(2)}) async-start(), calls=%async_computation.2 | async-start | bytes 8388608 | tf_op jit(solution)/shard_map/psum | solution.py:135
  36.7 36.2 %collective-permute-start.1 = (bf16[2,1024,256]{2,1,0:T(8,128)(2,1)}, bf16[2,1024,256]{2,1,0:T(8,128)(2,1)}, u32[]{:S(2)}, u32[]{:S(2)}) collective-permute-start(bf16[2,1024,256]{2,1,0:T(8,128)(2,1)} %pad_maximum_fusion.1), channel_id=1, source_target_pairs={{0,16},{8,24},{16,0},{24,8},{1,17},{9,25},{17,1},{25,9},{2,18},{10... | collective-permute-start | bytes 3145736 | tf_op jit(solution)/shard_map/ppermute | solution.py:25
  71.9 2.4 copy-start.11
  74.5 8.0 %copy-start.6 = (bf16[4,1024,256]{2,1,0:T(8,128)(2,1)}, bf16[4,1024,256]{2,1,0:T(8,128)(2,1)S(1)}, u32[]{:S(2)}) copy-start(bf16[4,1024,256]{2,1,0:T(8,128)(2,1)S(1)} %pad_maximum_fusion) | copy-start | bytes 6291460
  92.2 5.8 %copy-start.2 = (f32[2,1024,1024]{2,1,0:T(8,128)S(1)}, f32[2,1024,1024]{2,1,0:T(8,128)}, u32[]{:S(2)}) copy-start(f32[2,1024,1024]{2,1,0:T(8,128)} %get-tuple-element.756) | copy-start | bytes 25165828 | tf_op jit(solution)/shard_map/while
  92.2 6.1 %copy-start.16 = (f32[2,1024,128]{2,1,0:T(8,128)S(1)}, f32[2,1024,128]{2,1,0:T(8,128)}, u32[]{:S(2)}) copy-start(f32[2,1024,128]{2,1,0:T(8,128)} %get-tuple-element.792) | copy-start | bytes 3145732 | tf_op jit(solution)/shard_map/while
  102.0 1.0 copy-start.17
  112.8 5.8 %copy-start.2 = (f32[2,1024,1024]{2,1,0:T(8,128)S(1)}, f32[2,1024,1024]{2,1,0:T(8,128)}, u32[]{:S(2)}) copy-start(f32[2,1024,1024]{2,1,0:T(8,128)} %get-tuple-element.756) | copy-start | bytes 25165828 | tf_op jit(solution)/shard_map/while
  112.8 6.1 %copy-start.16 = (f32[2,1024,128]{2,1,0:T(8,128)S(1)}, f32[2,1024,128]{2,1,0:T(8,128)}, u32[]{:S(2)}) copy-start(f32[2,1024,128]{2,1,0:T(8,128)} %get-tuple-element.792) | copy-start | bytes 3145732 | tf_op jit(solution)/shard_map/while
  122.6 1.0 copy-start.17
  133.3 5.8 %copy-start.2 = (f32[2,1024,1024]{2,1,0:T(8,128)S(1)}, f32[2,1024,1024]{2,1,0:T(8,128)}, u32[]{:S(2)}) copy-start(f32[2,1024,1024]{2,1,0:T(8,128)} %get-tuple-element.756) | copy-start | bytes 25165828 | tf_op jit(solution)/shard_map/while
  133.3 6.1 %copy-start.16 = (f32[2,1024,128]{2,1,0:T(8,128)S(1)}, f32[2,1024,128]{2,1,0:T(8,128)}, u32[]{:S(2)}) copy-start(f32[2,1024,128]{2,1,0:T(8,128)} %get-tuple-element.792) | copy-start | bytes 3145732 | tf_op jit(solution)/shard_map/while
  143.1 1.0 copy-start.17
  153.8 5.8 %copy-start.2 = (f32[2,1024,1024]{2,1,0:T(8,128)S(1)}, f32[2,1024,1024]{2,1,0:T(8,128)}, u32[]{:S(2)}) copy-start(f32[2,1024,1024]{2,1,0:T(8,128)} %get-tuple-element.756) | copy-start | bytes 25165828 | tf_op jit(solution)/shard_map/while
  153.8 6.1 %copy-start.16 = (f32[2,1024,128]{2,1,0:T(8,128)S(1)}, f32[2,1024,128]{2,1,0:T(8,128)}, u32[]{:S(2)}) copy-start(f32[2,1024,128]{2,1,0:T(8,128)} %get-tuple-element.792) | copy-start | bytes 3145732 | tf_op jit(solution)/shard_map/while
  163.6 1.0 copy-start.17
  164.6 5.7 %copy-start.12 = (bf16[1024,2,128]{2,1,0:T(2,128)(2,1)S(1)}, bf16[1024,2,128]{2,1,0:T(2,128)(2,1)}, u32[]{:S(2)}) copy-start(bf16[1024,2,128]{2,1,0:T(2,128)(2,1)} %copy-done.11) | copy-start | bytes 1572868
  169.7 297.5 %reduce-scatter.3.cloned.1.call-start = ((), (), s32[]{:S(2)}) async-start(), calls=%async_computation.3 | async-start | bytes 5242880 | tf_op jit(solution)/shard_map/reduce_scatter | solution.py:198
  267.5 6.0 %copy-start.3 = (bf16[1024,2048]{1,0:T(8,128)(2,1)S(1)}, bf16[1024,2048]{1,0:T(8,128)(2,1)}, u32[]{:S(2)}) copy-start(bf16[1024,2048]{1,0:T(8,128)(2,1)} %param.13) | copy-start | bytes 12582916
  267.5 7.1 %copy-start.9 = (bf16[1024,2048]{1,0:T(8,128)(2,1)S(1)}, bf16[1024,2048]{1,0:T(8,128)(2,1)}, u32[]{:S(2)}) copy-start(bf16[1024,2048]{1,0:T(8,128)(2,1)} %param.17) | copy-start | bytes 12582916
  267.5 8.3 %copy-start.10 = (bf16[1024,2048]{1,0:T(8,128)(2,1)S(1)}, bf16[1024,2048]{1,0:T(8,128)(2,1)}, u32[]{:S(2)}) copy-start(bf16[1024,2048]{1,0:T(8,128)(2,1)} %all-reduce.2.cloned.1.call-done) | copy-start | bytes 12582916
  278.4 3.2 copy-start.5
  285.9 103.1 %copy-start.7 = (bf16[2,1024,128]{2,1,0:T(8,128)(2,1)S(1)}, bf16[2,1024,128]{2,1,0:T(8,128)(2,1)}, u32[]{:S(2)}) copy-start(bf16[2,1024,128]{2,1,0:T(8,128)(2,1)} %get-tuple-element.913) | copy-start | bytes 1572868
  289.7 5.8 %copy-start.8 = (bf16[2,1024,128]{1,2,0:T(8,128)(2,1)S(1)}, bf16[2,1024,128]{1,2,0:T(8,128)(2,1)}, u32[]{:S(2)}) copy-start(bf16[2,1024,128]{1,2,0:T(8,128)(2,1)} %get-tuple-element.895) | copy-start | bytes 1572868 | tf_op jit(solution)/shard_map/while
  315.5 5.8 %copy-start.8 = (bf16[2,1024,128]{1,2,0:T(8,128)(2,1)S(1)}, bf16[2,1024,128]{1,2,0:T(8,128)(2,1)}, u32[]{:S(2)}) copy-start(bf16[2,1024,128]{1,2,0:T(8,128)(2,1)} %get-tuple-element.895) | copy-start | bytes 1572868 | tf_op jit(solution)/shard_map/while
  341.3 5.8 %copy-start.8 = (bf16[2,1024,128]{1,2,0:T(8,128)(2,1)S(1)}, bf16[2,1024,128]{1,2,0:T(8,128)(2,1)}, u32[]{:S(2)}) copy-start(bf16[2,1024,128]{1,2,0:T(8,128)(2,1)} %get-tuple-element.895) | copy-start | bytes 1572868 | tf_op jit(solution)/shard_map/while
  367.1 5.8 %copy-start.8 = (bf16[2,1024,128]{1,2,0:T(8,128)(2,1)S(1)}, bf16[2,1024,128]{1,2,0:T(8,128)(2,1)}, u32[]{:S(2)}) copy-start(bf16[2,1024,128]{1,2,0:T(8,128)(2,1)} %get-tuple-element.895) | copy-start | bytes 1572868 | tf_op jit(solution)/shard_map/while
  389.0 137.3 %reduce-scatter.5.cloned.1.call-start = ((), (), s32[]{:S(2)}) async-start(), calls=%async_computation.4 | async-start | bytes 4718592 | tf_op jit(solution)/shard_map/reduce_scatter | solution.py:217
  389.2 8.5 %copy-start.18 = (bf16[2,1024,128]{2,1,0:T(8,128)(2,1)S(1)}, bf16[2,1024,128]{2,1,0:T(8,128)(2,1)}, u32[]{:S(2)}) copy-start(bf16[2,1024,128]{2,1,0:T(8,128)(2,1)} %get-tuple-element.852) | copy-start | bytes 1572868 | tf_op jit(solution)/shard_map/while
  406.8 8.3 %copy-start.18 = (bf16[2,1024,128]{2,1,0:T(8,128)(2,1)S(1)}, bf16[2,1024,128]{2,1,0:T(8,128)(2,1)}, u32[]{:S(2)}) copy-start(bf16[2,1024,128]{2,1,0:T(8,128)(2,1)} %get-tuple-element.852) | copy-start | bytes 1572868 | tf_op jit(solution)/shard_map/while
  424.5 8.3 %copy-start.18 = (bf16[2,1024,128]{2,1,0:T(8,128)(2,1)S(1)}, bf16[2,1024,128]{2,1,0:T(8,128)(2,1)}, u32[]{:S(2)}) copy-start(bf16[2,1024,128]{2,1,0:T(8,128)(2,1)} %get-tuple-element.852) | copy-start | bytes 1572868 | tf_op jit(solution)/shard_map/while
  442.2 8.3 %copy-start.18 = (bf16[2,1024,128]{2,1,0:T(8,128)(2,1)S(1)}, bf16[2,1024,128]{2,1,0:T(8,128)(2,1)}, u32[]{:S(2)}) copy-start(bf16[2,1024,128]{2,1,0:T(8,128)(2,1)} %get-tuple-element.852) | copy-start | bytes 1572868 | tf_op jit(solution)/shard_map/while
  467.1 3.9 copy-start.4
  467.1 4.1 copy-start.14
  475.9 50.4 %copy-start.21 = (f32[2048]{0:T(1024)S(1)}, f32[2048]{0:T(1024)}, u32[]{:S(2)}) copy-start(f32[2048]{0:T(1024)} %copy-done.20) | copy-start | bytes 24580
  475.9 52.0 %copy-start.19 = (bf16[128,2048]{1,0:T(8,128)(2,1)S(1)}, bf16[128,2048]{1,0:T(8,128)(2,1)}, u32[]{:S(2)}) copy-start(bf16[128,2048]{1,0:T(8,128)(2,1)} %param.18) | copy-start | bytes 1572868
  475.9 55.1 %copy-start.1 = (bf16[256,2048]{1,0:T(8,128)(2,1)S(1)}, bf16[256,2048]{1,0:T(8,128)(2,1)}, u32[]{:S(2)}) copy-start(bf16[256,2048]{1,0:T(8,128)(2,1)} %param.16) | copy-start | bytes 3145732
Sparse Core Ops, SparseCore 0:
  35.7 42.7 all-gather.2
  169.8 97.6 all-reduce.1
  389.1 52.6 reduce-scatter.2
  476.0 50.1 reduce-scatter.4
